TPU v7x, 32 devices: a whole 2x2x4 slice. The times are simulated.
32 devices in a mesh: expert: 4 (over x, core), tensor: 8 (over z, y).
Axes of the slice: x: 2, y: 2, z: 4, core: 2. Of those that a mesh axis runs over, the one named last changes fastest.
Arguments:
- tokens: bfloat16 [128, 7168], P('expert', 'tensor'), may hold values from -6 to 6
- routes: int32 [128, 8], P('expert'), may hold values from 0 to 15, all different within a row; in each aligned block of 128 rows (0 to 127, 128 to 255, ...) at most 128 rows name the same one
- gates: bfloat16 [128, 8], P('expert'), may hold values from 0.099609375 to 0.59765625
- w_gate: bfloat16 [16, 2048, 7168], P('expert', 'tensor'), may hold values from -0.0625 to 0.0625
- w_up: bfloat16 [16, 2048, 7168], P('expert', 'tensor'), may hold values from -0.0625 to 0.0625
- w_down: bfloat16 [16, 2048, 7168], P('expert', None, 'tensor'), may hold values from -0.125 to 0.125
Outputs:
- moe_out: bfloat16 [128, 7168], P('expert', 'tensor')
Inputs may be any that keep to these rules, and one draw needn't show every extreme that they name: `routes`: each row names 8 different experts. No expert is named by more than 128 of the 128 rows, and one expert is named by exactly 128 rows.
All inputs are finite; a program needn't handle non-finite values.
Results may differ from a plain program's by a relative error of at most 0.0049.
Values may be sent and summed in bfloat16 or wider, within the bound.
A program may use at most 128 MiB of HBM per device.

v0:
```python
import jax
import jax.numpy as jnp
from jax import lax
from jax.sharding import PartitionSpec as P

CAP = 128


def entering(value, axis, combine, identity):
    length, index = (lax.axis_size(axis), lax.axis_index(axis))
    everything = lax.all_gather(value, axis)
    start = jnp.broadcast_to(jnp.asarray(identity, value.dtype), value.shape)

    def lap(k, before):
        reached = k < index
        new = combine(before, everything[k])
        return jnp.where(reached, new, before)

    return lax.fori_loop(0, length, lap, start)


def add_counts(earlier, later):
    return earlier + later


def on_device(tokens, routes, gates, w_gate, w_up, w_down):
    exp_dev = w_gate.shape[0]
    experts = exp_dev * lax.axis_size("expert")
    group_index = lax.axis_index("expert")
    expert_ids = jnp.arange(experts, dtype=jnp.int32)
    route_hits = routes[:, :, None] == expert_ids[None, None, :]
    member = jnp.sum(route_hits.astype(jnp.int32), axis=1)
    counts = jnp.sum(member, axis=0)
    offset = entering(counts, "expert", add_counts, jnp.zeros_like(counts))
    before = jnp.cumsum(member, axis=0) - member + offset[None, :]
    own_slot = jnp.sum(jnp.where(route_hits, before[:, None, :], 0), axis=2).astype(jnp.int32)
    all_routes, all_slots = (
        lax.all_gather(routes, "expert", axis=0, tiled=True),
        lax.all_gather(own_slot, "expert", axis=0, tiled=True),
    )
    row_block, all_gates = (
        lax.all_gather(tokens, "expert", axis=0, tiled=True),
        lax.all_gather(gates, "expert", axis=0, tiled=True),
    )
    gathered = lax.all_gather(row_block, "tensor", axis=1, tiled=True)
    local_ids = all_routes - group_index * exp_dev
    is_local = (local_ids >= 0) & (local_ids < exp_dev)
    slot_id = jnp.where(is_local, local_ids * CAP + all_slots, -1)
    slot_range = jnp.arange(exp_dev * CAP, dtype=jnp.int32)
    matches = slot_id[:, :, None] == slot_range[None, None, :]
    picked = jnp.any(matches, axis=1).astype(jnp.bfloat16)
    mixing = jnp.sum(jnp.where(matches, all_gates.astype(jnp.float32)[:, :, None], 0.0), axis=1)
    slot_rows = lax.dot_general(
        picked, gathered, (((0,), (0,)), ((), ())), preferred_element_type=jnp.float32
    ).astype(jnp.bfloat16)
    slot_rows = slot_rows.reshape(exp_dev, CAP, gathered.shape[1])
    gate_proj = jnp.einsum("ecd,efd->ecf", slot_rows, w_gate, preferred_element_type=jnp.float32)
    up_proj = jnp.einsum("ecd,efd->ecf", slot_rows, w_up, preferred_element_type=jnp.float32)
    hidden = (jax.nn.silu(gate_proj) * up_proj).astype(jnp.bfloat16)
    expert_out = jnp.einsum(
        "ecf,efd->ecd",
        lax.all_gather(hidden, "tensor", axis=2, tiled=True),
        w_down,
        preferred_element_type=jnp.float32,
    )
    expert_out = expert_out.reshape(exp_dev * CAP, w_down.shape[2])
    partial_value = jnp.dot(mixing, expert_out, precision=lax.Precision.HIGHEST)
    result = lax.psum_scatter(partial_value, "expert", scatter_dimension=0, tiled=True)
    return result.astype(jnp.bfloat16)


def solution(mesh):
    placed = (
        P("expert", "tensor"),
        P("expert", None),
        P("expert", None),
        P("expert", "tensor", None),
        P("expert", "tensor", None),
        P("expert", None, "tensor"),
    )
    return jax.shard_map(
        on_device, mesh=mesh, in_specs=placed, out_specs=P("expert", "tensor"), check_vma=False
    )
```

profile of v0, /device:TPU:0, one launch (start us, length us, event | category | flops | bytes accessed | tf_op | source)
XLA Modules:
  0.0 181.3 jit_solution(15544654380891682984)
XLA Ops:
  6.5 8.7 %all_gather.29 = bf16[128,896]{1,0:T(8,128)(2,1)} all-gather(bf16[32,896]{1,0:T(8,128)(2,1)} %param.8), channel_id=1, replica_groups=mesh['expert'=4,'tensor'=8] {'expert'}, dimensions={0}, use_global_device_ids=true | all-gather | bytes 286720 | tf_op jit(solution)/shard_map/all_gather | solution.py:42
  15.3 1.2 dynamic-slice
  17.2 0.8 convert_reduce_fusion
  18.0 0.2 dynamic-update-slice
  18.2 4.3 %all-reduce = s32[64]{0:T(128)S(1)} all-reduce(s32[64]{0:T(128)S(1)} %dynamic-update-slice), channel_id=2, replica_groups=mesh['expert'=4,'tensor'=8] {'expert'}, use_global_device_ids=true, to_apply=%add | all-reduce | flops 64 | bytes 512
  22.5 0.1 reshape.32
  22.7 0.1 while.14
  22.9 0.7 select_reduce_fusion.1
  23.7 5.2 %all-gather.2 = s32[4,32,8]{1,2,0:T(8,128)S(1)} all-gather(s32[1,32,8]{1,2,0:T(8,128)S(1)} %bitcast.29), channel_id=1, replica_groups=mesh['expert'=4,'tensor'=8] {'expert'}, dimensions={0}, use_global_device_ids=true | all-gather | bytes 5120 | tf_op jit(solution)/shard_map/all_gather | solution.py:39
  28.9 5.3 %all-gather.1 = s32[4,32,8]{1,2,0:T(8,128)S(1)} all-gather(s32[1,32,8]{1,2,0:T(8,128)} %bitcast.28), channel_id=1, replica_groups=mesh['expert'=4,'tensor'=8] {'expert'}, dimensions={0}, use_global_device_ids=true | all-gather | bytes 5120 | tf_op jit(solution)/shard_map/all_gather | solution.py:38
  34.2 0.1 copy.25
  34.3 0.7 fusion
  35.0 27.3 %all-gather.7.cloned.1.call-done = bf16[128,7168]{1,0:T(8,128)(2,1)} async-done(((bf16[128,896]{1,0:T(8,128)(2,1)}), bf16[128,7168]{1,0:T(8,128)(2,1)}) %all-gather.7.cloned.1.call-update) | async-done | bytes 1835024 | tf_op jit(solution)/shard_map/all_gather | solution.py:45
  62.3 6.6 %convolution_convert_fusion = bf16[512,7168]{1,0:T(8,128)(2,1)} fusion(pred[128,512]{1,0:T(8,128)(4,1)S(1)} %fusion, bf16[128,7168]{1,0:T(8,128)(2,1)} %all-gather.7.cloned.1.call-done), kind=kOutput, calls=%fused_computation.2 | convolution fusion | flops 943194112 | bytes 9240576 | tf_op jit(solution)/shard_map/dot_general | solution.py:53
  68.9 12.3 %fusion.2 = f32[4,128,256]{2,1,0:T(8,128)S(1)} fusion(bf16[4,128,7168]{2,1,0:T(8,128)(2,1)} %bitcast.22, bf16[4,256,7168]{2,1,0:T(8,128)(2,1)} %param.11), kind=kOutput, calls=%fused_computation.14 | convolution fusion | flops 1879048192 | bytes 22544384 | tf_op jit(solution)/shard_map/ecd,efd->ecf/dot_general | solution.py:57
  81.2 13.0 %fusion.1 = bf16[4,128,256]{2,1,0:T(8,128)(2,1)} fusion(bf16[4,128,7168]{2,1,0:T(8,128)(2,1)} %bitcast.23, bf16[4,256,7168]{2,1,0:T(8,128)(2,1)} %param.12, f32[4,128,256]{2,1,0:T(8,128)S(1)} %fusion.2), kind=kOutput, calls=%fused_computation.7 | convolution fusion | flops 1879834624 | bytes 22806528 | tf_op jit(solution)/shard_map/ecd,efd->ecf/dot_general | solution.py:58
  94.3 5.4 %all-gather.3 = bf16[4,32,8]{1,2,0:T(8,128)(2,1)S(1)} all-gather(bf16[1,32,8]{1,2,0:T(8,128)(2,1)S(1)} %bitcast.30), channel_id=1, replica_groups=mesh['expert'=4,'tensor'=8] {'expert'}, dimensions={0}, use_global_device_ids=true | all-gather | bytes 2560 | tf_op jit(solution)/shard_map/all_gather | solution.py:43
  99.6 0.1 copy.26
  99.7 0.7 select_reduce_fusion
  100.4 43.1 %all-gather.9.cloned.1.call-done = bf16[4,128,2048]{2,1,0:T(8,128)(2,1)} async-done(((bf16[4,128,256]{2,1,0:T(8,128)(2,1)}), bf16[4,128,2048]{2,1,0:T(8,128)(2,1)}) %all-gather.9.cloned.1.call-update) | async-done | bytes 2097168 | tf_op jit(solution)/shard_map/all_gather | solution.py:62
  143.5 8.2 %fusion.3 = f32[4,128,896]{2,1,0:T(8,128)S(1)} fusion(bf16[4,128,2048]{2,1,0:T(8,128)(2,1)} %all-gather.9.cloned.1.call-done, bf16[4,2048,896]{2,1,0:T(8,128)(2,1)} %param.13), kind=kOutput, calls=%fused_computation.15 | convolution fusion | flops 1879048192 | bytes 18612224 | tf_op jit(solution)/shard_map/ecf,efd->ecd/dot_general | solution.py:60
  151.7 2.0 %fusion.4 = f32[128,896]{1,0:T(8,128)} fusion(f32[128,512]{1,0:T(8,128)S(1)} %select_reduce_fusion, f32[512,896]{1,0:T(8,128)S(1)} %bitcast.24), kind=kOutput, calls=%fused_computation.16 | convolution fusion | flops 704643072 | bytes 2555904 | tf_op jit(solution)/shard_map/dot_general | solution.py:67
  153.7 19.5 %reduce-scatter.2.cloned.1.call-done = f32[32,896]{1,0:T(8,128)} async-done(((f32[128,896]{1,0:T(8,128)}), f32[32,896]{1,0:T(8,128)}) %reduce-scatter.2.cloned.1.call-update) | async-done | bytes 114704 | tf_op jit(solution)/shard_map/reduce_scatter | solution.py:68
  173.2 1.5 convert_element_type.20
  (19 shorter events, 0.4 us)
Async XLA Ops:
  6.5 55.8 %all-gather.7.cloned.1.call-start = ((), (), s32[]{:S(2)}) async-start(), calls=%async_computation.1 | async-start | bytes 2064384 | tf_op jit(solution)/shard_map/all_gather | solution.py:45
  15.3 128.3 %all-gather.9.cloned.1.call-start = ((), (), s32[]{:S(2)}) async-start(), calls=%async_computation.2 | async-start | bytes 2359296 | tf_op jit(solution)/shard_map/all_gather | solution.py:62
  81.2 13.1 %copy-start = (bf16[32,8]{0,1:T(8,128)(2,1)S(1)}, bf16[32,8]{0,1:T(8,128)(2,1)}, u32[]{:S(2)}) copy-start(bf16[32,8]{0,1:T(8,128)(2,1)} %param.10) | copy-start | bytes 1540
  94.2 79.0 %reduce-scatter.2.cloned.1.call-start = ((), (), s32[]{:S(2)}) async-start(), calls=%async_computation.3 | async-start | bytes 573440 | tf_op jit(solution)/shard_map/reduce_scatter | solution.py:68
Sparse Core Ops, SparseCore 0:
  15.4 46.8 all-gather.6
  94.3 49.1 all-gather.8
  153.8 19.3 reduce-scatter.1
where the time goes:
time: 182 us; the launch traced here: 181 us
  waiting for transfers between devices  90 us (49%)
  matrix products  42 us (23%)
  blocking collectives  28.9 us (16%)
  between operations  13.8 us (8%)
  other arithmetic  4.59 us (3%)
  local copies, waits for them, and re-layouts  1.88 us (1%)
    all_gather x1, waiting for transfers between devices, on_device(): lax.all_gather(hidden, 'tensor', axis=2, tiled=True)  43.1 us
    all_gather x1, waiting for transfers between devices, on_device(): gathered = lax.all_gather(row_block, 'tensor', axis=1, tiled=True)  27.3 us
    reduce_scatter x1, waiting for transfers between devices, on_device(): lax.psum_scatter(partial_value, 'expert', scatter_dimension=0, tiled=True)  19.5 us
    dot_general x1, matrix products, on_device(): jnp.einsum('ecd,efd->ecf', slot_rows, w_up, preferred_element_type=jnp.fl...  13 us
    dot_general x1, matrix products, on_device(): jnp.einsum('ecd,efd->ecf', slot_rows, w_gate, preferred_element_type=jnp....  12.3 us
    all_gather x1, blocking collectives, on_device(): lax.all_gather(tokens, 'expert', axis=0, tiled=True)  8.71 us
    dot_general x1, matrix products, on_device(): jnp.einsum('ecf,efd->ecd', lax.all_gather(hidden, 'tensor', axis=2, tiled...  8.16 us
    dot_general x1, matrix products, on_device(): lax.dot_general(picked, gathered, (((0,), (0,)), ((), ())), preferred_ele...  6.58 us
  transfers between devices with their start and end apart: 3, of which 3 were waited for; matrix products, arithmetic and copies ran while one was open for 3% of the time, Pallas kernels for 0%

commit v1 on v0

--- a/solution.py
+++ b/solution.py
@@ -42,7 +42,7 @@
         lax.all_gather(tokens, "expert", axis=0, tiled=True),
         lax.all_gather(gates, "expert", axis=0, tiled=True),
     )
-    gathered = lax.all_gather(row_block, "tensor", axis=1, tiled=True)
+    gathered = jnp.concatenate(lax.all_gather(row_block, "tensor"), axis=1)
     local_ids = all_routes - group_index * exp_dev
     is_local = (local_ids >= 0) & (local_ids < exp_dev)
     slot_id = jnp.where(is_local, local_ids * CAP + all_slots, -1)

time: 182 us -> 183 us (level)
  local copies, waits for them, and re-layouts: 1.88 us -> 5.12 us
    reshape x0 -> x1, local copies, waits for them, and re-layouts: none -> 3.16 us  [on_device(): gathered = jnp.concatenate(lax.all_gather(row_block, 'tensor'), axis=1)]
where the time goes in v1:
time: 183 us
  waiting for transfers between devices  89.5 us (49%)
  matrix products  40.5 us (22%)
  blocking collectives  28.9 us (16%)
  between operations  13.9 us (8%)
  local copies, waits for them, and re-layouts  5.12 us (3%)
  other arithmetic  4.59 us (3%)
    all_gather x1, waiting for transfers between devices, on_device(): lax.all_gather(hidden, 'tensor', axis=2, tiled=True)  43 us
    all_gather x1, waiting for transfers between devices, on_device(): gathered = jnp.concatenate(lax.all_gather(row_block, 'tensor'), axis=1)  27 us
    reduce_scatter x1, waiting for transfers between devices, on_device(): lax.psum_scatter(partial_value, 'expert', scatter_dimension=0, tiled=True)  19.5 us
    dot_general x1, matrix products, on_device(): jnp.einsum('ecd,efd->ecf', slot_rows, w_up, preferred_element_type=jnp.fl...  13 us
    dot_general x1, matrix products, on_device(): jnp.einsum('ecd,efd->ecf', slot_rows, w_gate, preferred_element_type=jnp....  12.3 us
    all_gather x1, blocking collectives, on_device(): lax.all_gather(tokens, 'expert', axis=0, tiled=True)  8.72 us
    dot_general x1, matrix products, on_device(): jnp.einsum('ecf,efd->ecd', lax.all_gather(hidden, 'tensor', axis=2, tiled...  8.16 us
    all_gather x1, blocking collectives, on_device(): lax.all_gather(gates, 'expert', axis=0, tiled=True)  5.37 us
  transfers between devices with their start and end apart: 3, of which 3 were waited for; matrix products, arithmetic and copies ran while one was open for 3% of the time, Pallas kernels for 0%

profile of v1, /device:TPU:0, one launch (start us, length us, event | category | flops | bytes accessed | tf_op | source)
XLA Modules:
  0.0 182.7 jit_solution(17152860726150036627)
XLA Ops:
  6.5 8.7 %all_gather.32 = bf16[128,896]{1,0:T(8,128)(2,1)} all-gather(bf16[32,896]{1,0:T(8,128)(2,1)} %param.8), channel_id=1, replica_groups=mesh['expert'=4,'tensor'=8] {'expert'}, dimensions={0}, use_global_device_ids=true | all-gather | bytes 286720 | tf_op jit(solution)/shard_map/all_gather | solution.py:42
  15.4 1.3 dynamic-slice
  17.4 0.8 convert_reduce_fusion
  18.2 0.2 dynamic-update-slice
  18.4 4.3 %all-reduce = s32[64]{0:T(128)S(1)} all-reduce(s32[64]{0:T(128)S(1)} %dynamic-update-slice), channel_id=2, replica_groups=mesh['expert'=4,'tensor'=8] {'expert'}, use_global_device_ids=true, to_apply=%add | all-reduce | flops 64 | bytes 512
  22.7 0.1 reshape.40
  22.9 0.1 while.14
  23.1 0.7 select_reduce_fusion.1
  23.9 5.2 %all-gather.3 = s32[4,32,8]{1,2,0:T(8,128)S(1)} all-gather(s32[1,32,8]{1,2,0:T(8,128)S(1)} %bitcast.34), channel_id=1, replica_groups=mesh['expert'=4,'tensor'=8] {'expert'}, dimensions={0}, use_global_device_ids=true | all-gather | bytes 5120 | tf_op jit(solution)/shard_map/all_gather | solution.py:39
  29.1 5.3 %all-gather.2 = s32[4,32,8]{1,2,0:T(8,128)S(1)} all-gather(s32[1,32,8]{1,2,0:T(8,128)} %bitcast.33), channel_id=1, replica_groups=mesh['expert'=4,'tensor'=8] {'expert'}, dimensions={0}, use_global_device_ids=true | all-gather | bytes 5120 | tf_op jit(solution)/shard_map/all_gather | solution.py:38
  34.5 0.7 fusion
  35.2 27.0 %all-gather.10.cloned.1.call-done = bf16[1024,896]{1,0:T(8,128)(2,1)} async-done(((bf16[128,896]{1,0:T(8,128)(2,1)}), bf16[1024,896]{1,0:T(8,128)(2,1)}) %all-gather.10.cloned.1.call-update) | async-done | bytes 1835024 | tf_op jit(solution)/shard_map/all_gather | solution.py:45
  62.2 3.2 %copy.32 = bf16[128,8,896]{0,2,1:T(8,128)(2,1)S(1)} copy(bf16[128,8,896]{2,0,1:T(8,128)(2,1)} %bitcast.29) | data formatting | bytes 3670016 | tf_op jit(solution)/shard_map/reshape | solution.py:45
  65.3 5.1 %convolution_convert_fusion = bf16[512,7168]{1,0:T(8,128)(2,1)} fusion(bf16[128,7168]{0,1:T(8,128)(2,1)S(1)} %bitcast.28, pred[128,512]{1,0:T(8,128)(4,1)S(1)} %fusion), kind=kOutput, calls=%fused_computation.2 | convolution fusion | flops 943259648 | bytes 9240576 | tf_op jit(solution)/shard_map/dot_general | solution.py:53
  70.4 12.3 %fusion.3 = f32[4,128,256]{2,1,0:T(8,128)S(1)} fusion(bf16[4,128,7168]{2,1,0:T(8,128)(2,1)} %bitcast.25, bf16[4,256,7168]{2,1,0:T(8,128)(2,1)} %param.11), kind=kOutput, calls=%fused_computation.15 | convolution fusion | flops 1879048192 | bytes 22544384 | tf_op jit(solution)/shard_map/ecd,efd->ecf/dot_general | solution.py:57
  82.7 13.0 %fusion.1 = bf16[4,128,256]{2,1,0:T(8,128)(2,1)} fusion(bf16[4,128,7168]{2,1,0:T(8,128)(2,1)} %bitcast.26, bf16[4,256,7168]{2,1,0:T(8,128)(2,1)} %param.12, f32[4,128,256]{2,1,0:T(8,128)S(1)} %fusion.3), kind=kOutput, calls=%fused_computation.7 | convolution fusion | flops 1879834624 | bytes 22806528 | tf_op jit(solution)/shard_map/ecd,efd->ecf/dot_general | solution.py:58
  95.8 5.4 %all-gather.4 = bf16[4,32,8]{1,2,0:T(8,128)(2,1)S(1)} all-gather(bf16[1,32,8]{1,2,0:T(8,128)(2,1)S(1)} %bitcast.35), channel_id=1, replica_groups=mesh['expert'=4,'tensor'=8] {'expert'}, dimensions={0}, use_global_device_ids=true | all-gather | bytes 2560 | tf_op jit(solution)/shard_map/all_gather | solution.py:43
  101.1 0.1 copy.34
  101.2 0.7 select_reduce_fusion
  101.9 43.0 %all-gather.8.cloned.1.call-done = bf16[4,128,2048]{2,1,0:T(8,128)(2,1)} async-done(((bf16[4,128,256]{2,1,0:T(8,128)(2,1)}), bf16[4,128,2048]{2,1,0:T(8,128)(2,1)}) %all-gather.8.cloned.1.call-update) | async-done | bytes 2097168 | tf_op jit(solution)/shard_map/all_gather | solution.py:62
  144.9 8.2 %fusion.4 = f32[4,128,896]{2,1,0:T(8,128)S(1)} fusion(bf16[4,128,2048]{2,1,0:T(8,128)(2,1)} %all-gather.8.cloned.1.call-done, bf16[4,2048,896]{2,1,0:T(8,128)(2,1)} %param.13), kind=kOutput, calls=%fused_computation.16 | convolution fusion | flops 1879048192 | bytes 18612224 | tf_op jit(solution)/shard_map/ecf,efd->ecd/dot_general | solution.py:60
  153.1 2.0 %fusion.5 = f32[128,896]{1,0:T(8,128)} fusion(f32[128,512]{1,0:T(8,128)S(1)} %select_reduce_fusion, f32[512,896]{1,0:T(8,128)S(1)} %bitcast.27), kind=kOutput, calls=%fused_computation.17 | convolution fusion | flops 704643072 | bytes 2555904 | tf_op jit(solution)/shard_map/dot_general | solution.py:67
  155.1 19.5 %reduce-scatter.2.cloned.1.call-done = f32[32,896]{1,0:T(8,128)} async-done(((f32[128,896]{1,0:T(8,128)}), f32[32,896]{1,0:T(8,128)}) %reduce-scatter.2.cloned.1.call-update) | async-done | bytes 114704 | tf_op jit(solution)/shard_map/reduce_scatter | solution.py:68
  174.6 1.5 convert_element_type.20
  (20 shorter events, 0.5 us)
Async XLA Ops:
  6.5 55.6 %all-gather.10.cloned.1.call-start = ((), (), s32[]{:S(2)}) async-start(), calls=%async_computation.3 | async-start | bytes 2064384 | tf_op jit(solution)/shard_map/all_gather | solution.py:45
  15.3 129.6 %all-gather.8.cloned.1.call-start = ((), (), s32[]{:S(2)}) async-start(), calls=%async_computation.1 | async-start | bytes 2359296 | tf_op jit(solution)/shard_map/all_gather | solution.py:62
  82.7 13.1 %copy-start = (bf16[32,8]{0,1:T(8,128)(2,1)S(1)}, bf16[32,8]{0,1:T(8,128)(2,1)}, u32[]{:S(2)}) copy-start(bf16[32,8]{0,1:T(8,128)(2,1)} %param.10) | copy-start | bytes 1540
  95.7 78.9 %reduce-scatter.2.cloned.1.call-start = ((), (), s32[]{:S(2)}) async-start(), calls=%async_computation.2 | async-start | bytes 573440 | tf_op jit(solution)/shard_map/reduce_scatter | solution.py:68
Sparse Core Ops, SparseCore 0:
  15.4 46.7 all-gather.9
  95.8 49.0 all-gather.7
  155.2 19.3 reduce-scatter.1
